TPU v7x, 32 devices: a whole 2x2x4 slice. The times are simulated.
32 devices in a mesh: section: 4 (over y, x), mp: 8 (over z, core).
Axes of the slice: x: 2, y: 2, z: 4, core: 2. Of those that a mesh axis runs over, the one named last changes fastest.
Arguments:
- stream: bfloat16 [512, 4096], P(('section', 'mp')), may hold values from -6 to 6
- ffn_gain: float32 [4096], replicated, may hold values from 0.25 to 1.75
- router_weight: bfloat16 [4096, 4], replicated, may hold values from -0.1875 to 0.1875
- expert_ids: int32 [512, 2], P(('section', 'mp')), may hold values from 0 to 3, all different within a row; in each aligned block of 16 rows (0 to 15, 16 to 31, ...) at most 12 rows name the same one
- w_gate: bfloat16 [4, 4096, 14336], P('section', None, 'mp'), may hold values from -0.09375 to 0.09375
- w_up: bfloat16 [4, 4096, 14336], P('section', None, 'mp'), may hold values from -0.09375 to 0.09375
- w_down: bfloat16 [4, 14336, 4096], P('section', 'mp'), may hold values from -0.09375 to 0.09375
- attn_gain: float32 [4096], replicated, may hold values from 0.25 to 1.75
- w_kv: bfloat16 [4096, 2048], P(None, 'mp'), may hold values from -0.09375 to 0.09375
Outputs:
- stream_out: bfloat16 [512, 4096], P(('section', 'mp'))
- kv_decode: bfloat16 [512, 2048], P('section', 'mp')
Inputs may be any that keep to these rules, and one draw needn't show every extreme that they name: `expert_ids`: each row names two different experts. Among the rows of one device no expert is named more than 12 times, a bound that some block reaches.
All inputs are finite; a program needn't handle non-finite values.
Results may differ from a plain program's by a relative error of at most 0.02.
Values may be sent and summed in bfloat16 or wider, within the bound.
A program may use at most 128 MiB of HBM per device.

v0:
```python
import jax
import jax.numpy as jnp
from jax import lax
from jax.sharding import PartitionSpec as P

epsilon = 1e-05


def shifted(value, axis, steps):
    count = lax.axis_size(axis)
    pairs = [(source, (source + steps) % count) for source in range(count)]
    return lax.ppermute(value, axis, pairs)


def normalize(values, scale_gain):
    floats = values.astype(jnp.float32)
    return (
        floats * lax.rsqrt(jnp.mean(floats * floats, axis=-1, keepdims=True) + epsilon) * scale_gain
    )


def body(stream, ffn_gain, router_weight, expert_ids, w_gate, w_up, w_down, attn_gain, w_kv):
    own_rows = stream.shape[0]
    model_width = stream.shape[1]
    experts = router_weight.shape[1]
    capacity = min(own_rows, 3 * own_rows // experts)
    normed = normalize(stream, ffn_gain).astype(jnp.bfloat16)
    logits = jnp.dot(normed, router_weight, preferred_element_type=jnp.float32)
    onehot = expert_ids[:, :, None] == jnp.arange(experts, dtype=jnp.int32)[None, None, :]
    chosen = jnp.sum(jnp.where(onehot, logits[:, None, :], jnp.float32(0.0)), axis=-1)
    share_first = jax.nn.sigmoid(chosen[:, 0] - chosen[:, 1])
    flat_hits = onehot.reshape(own_rows * 2, experts).astype(jnp.int32)
    before = jnp.cumsum(flat_hits, axis=0) - flat_hits
    slot_index = jnp.sum(before * flat_hits, axis=-1)
    expert_flat = expert_ids.reshape(-1)
    route_table = (
        expert_flat[None, None, :] == jnp.arange(experts, dtype=jnp.int32)[:, None, None]
    ) & (slot_index[None, None, :] == jnp.arange(capacity, dtype=jnp.int32)[None, :, None])
    route_table = route_table.astype(jnp.bfloat16)
    repeated = jnp.repeat(normed, 2, axis=0)
    buffer = jnp.einsum(
        "ecr,rd->ecd", route_table, repeated, preferred_element_type=jnp.float32
    ).astype(jnp.bfloat16)
    arrived = lax.all_to_all(buffer, "section", split_axis=0, concat_axis=0, tiled=True)
    inbound = arrived.reshape(experts * capacity, model_width)
    gate_weight = w_gate[0]
    up_weight = w_up[0]
    down_weight = w_down[0]
    block_rows = lax.all_gather(inbound, "mp", axis=0, tiled=True)
    gate_part = jnp.dot(block_rows, gate_weight, preferred_element_type=jnp.float32)
    up_part = jnp.dot(block_rows, up_weight, preferred_element_type=jnp.float32)
    hidden_all = (jax.nn.silu(gate_part) * up_part).astype(jnp.bfloat16)
    block_rows = hidden_all
    summed = lax.psum_scatter(
        jnp.dot(block_rows, down_weight, preferred_element_type=jnp.float32).astype(jnp.bfloat16),
        "mp",
        scatter_dimension=0,
        tiled=True,
    )
    results = summed.reshape(experts, capacity, model_width)
    returned = lax.all_to_all(results, "section", split_axis=0, concat_axis=0, tiled=True)
    picked = jnp.einsum("ecr,ecd->rd", route_table, returned, preferred_element_type=jnp.float32)
    picked = picked.reshape(own_rows, 2, model_width)
    updated = (
        stream.astype(jnp.float32)
        + share_first[:, None] * picked[:, 0]
        + (1.0 - share_first)[:, None] * picked[:, 1]
    )
    stream_out = updated.astype(jnp.bfloat16)
    attn_input = normalize(stream_out, attn_gain).astype(jnp.bfloat16)
    kv_local = jnp.dot(
        lax.all_gather(attn_input, "mp", axis=0, tiled=True),
        w_kv,
        preferred_element_type=jnp.float32,
    ).astype(jnp.bfloat16)
    kv_decode = shifted(kv_local, "section", 1)
    return (stream_out, kv_decode)


def solution(mesh):
    in_specs = (
        P(("section", "mp"), None),
        P(),
        P(),
        P(("section", "mp"), None),
        P("section", None, "mp"),
        P("section", None, "mp"),
        P("section", "mp", None),
        P(),
        P(None, "mp"),
    )
    out_specs = (P(("section", "mp"), None), P("section", "mp"))
    return jax.shard_map(body, mesh=mesh, in_specs=in_specs, out_specs=out_specs, check_vma=False)
```

profile of v0, /device:TPU:0, one launch (start us, length us, event | category | flops | bytes accessed | tf_op | source)
XLA Modules:
  0.0 191.3 jit_solution(9461943533034778147)
XLA Ops:
  7.2 0.9 copy.21
  8.3 1.1 fusion.21
  9.6 1.0 fusion.23
  10.9 0.3 convolution_convert_fusion
  11.2 13.5 %all_to_all.10 = bf16[4,12,4096]{2,1,0:T(8,128)(2,1)S(1)} all-to-all(bf16[4,12,4096]{2,1,0:T(8,128)(2,1)S(1)} %convolution_convert_fusion), channel_id=1, replica_groups=mesh['section'=4,'mp'=8] {'section'}, dimensions={0} | all-to-all | bytes 786432 | tf_op jit(solution)/shard_map/all_to_all | solution.py:44
  24.7 0.8 reshape.88
  25.7 38.0 %all-gather.3.cloned.1.call-done = bf16[384,4096]{1,0:T(8,128)(2,1)} async-done(((bf16[48,4096]{1,0:T(8,128)(2,1)}), bf16[384,4096]{1,0:T(8,128)(2,1)}) %all-gather.3.cloned.1.call-update) | async-done | bytes 3145744 | tf_op jit(solution)/shard_map/all_gather | solution.py:49
  63.7 12.9 %fusion.4 = f32[384,1792]{1,0:T(8,128)} fusion(bf16[384,4096]{1,0:T(8,128)(2,1)} %all-gather.3.cloned.1.call-done, bf16[1,4096,1792]{2,1,0:T(8,128)(2,1)} %param.13), kind=kOutput, calls=%fused_computation.4 | convolution fusion | flops 5637144576 | bytes 20578304 | tf_op jit(solution)/shard_map/dot_general | solution.py:50
  76.6 25.0 %fusion.6 = bf16[384,4096]{1,0:T(8,128)(2,1)} fusion(bf16[1,1792,4096]{2,1,0:T(8,128)(2,1)} %param.15, bf16[384,4096]{1,0:T(8,128)(2,1)} %all-gather.3.cloned.1.call-done, bf16[1,4096,1792]{2,1,0:T(8,128)(2,1)} %param.14, f32[384,1792]{1,0:T(8,128)} %fusion.4), kind=kOutput, calls=%fused_computation.6 | convolution fusion | flops 11279990784 | bytes 38404096 | tf_op jit(solution)/shard_map/dot_general | solution.py:55
  101.6 0.7 copy-done.5
  102.5 38.6 %reduce-scatter.2.cloned.1.call-done = bf16[48,4096]{1,0:T(8,128)(2,1)} async-done(((bf16[384,4096]{1,0:T(8,128)(2,1)}), bf16[48,4096]{1,0:T(8,128)(2,1)}) %reduce-scatter.2.cloned.1.call-update) | async-done | bytes 393232 | tf_op jit(solution)/shard_map/reduce_scatter | solution.py:54
  141.1 1.9 reshape.89
  143.0 3.7 %all-to-all-start.1 = ((bf16[4,12,4096]{2,1,0:T(8,128)(2,1)}), bf16[4,12,4096]{2,1,0:T(8,128)(2,1)S(1)}, u32[]{:S(2)}, u32[]{:S(2)}) async-start(bf16[4,12,4096]{2,1,0:T(8,128)(2,1)} %reshape.89), calls=%async_computation.2 | async-start | bytes 1048576 | tf_op jit(solution)/shard_map/all_to_all | solution.py:61
  146.7 6.5 %all-to-all-done.1 = bf16[4,12,4096]{2,1,0:T(8,128)(2,1)S(1)} async-done(((bf16[4,12,4096]{2,1,0:T(8,128)(2,1)}), bf16[4,12,4096]{2,1,0:T(8,128)(2,1)S(1)}, u32[]{:S(2)}, u32[]{:S(2)}) %all-to-all-start.1) | async-done | bytes 393248 | tf_op jit(solution)/shard_map/all_to_all | solution.py:61
  153.2 0.3 convolution_bitcast_fusion
  153.5 0.3 reshape.90
  153.8 0.5 fusion.37
  154.4 0.4 fusion.18
  154.8 0.7 fusion.20
  155.6 21.7 %all-gather.5.cloned.1.call-done = bf16[128,4096]{1,0:T(8,128)(2,1)} async-done(((bf16[16,4096]{1,0:T(8,128)(2,1)}), bf16[128,4096]{1,0:T(8,128)(2,1)}) %all-gather.5.cloned.1.call-update) | async-done | bytes 1048592 | tf_op jit(solution)/shard_map/all_gather | solution.py:72
  177.2 1.7 convolution_convert_fusion.1
  178.9 1.5 collective-permute-start
  180.4 3.7 %collective-permute-done = bf16[128,256]{1,0:T(8,128)(2,1)S(1)} collective-permute-done((bf16[128,256]{1,0:T(8,128)(2,1)S(1)}, bf16[128,256]{1,0:T(8,128)(2,1)S(1)}, u32[]{:S(2)}, u32[]{:S(2)}) %collective-permute-start) | collective-permute-done | bytes 65568 | tf_op jit(solution)/shard_map/ppermute | solution.py:12
  184.1 0.6 copy.39
  (30 shorter events, 1.1 us)
Async XLA Ops:
  7.2 170.1 %copy-start = (bf16[4096,256]{1,0:T(8,128)(2,1)S(1)}, bf16[4096,256]{1,0:T(8,128)(2,1)}, u32[]{:S(2)}) copy-start(bf16[4096,256]{1,0:T(8,128)(2,1)} %param.17) | copy-start | bytes 6291460
  7.2 56.5 %all-gather.3.cloned.1.call-start = ((), (), s32[]{:S(2)}) async-start(), calls=%async_computation.3 | async-start | bytes 3538944 | tf_op jit(solution)/shard_map/all_gather | solution.py:49
  25.6 115.5 %reduce-scatter.2.cloned.1.call-start = ((), (), s32[]{:S(2)}) async-start(), calls=%async_computation.4 | async-start | bytes 3538944 | tf_op jit(solution)/shard_map/reduce_scatter | solution.py:54
  101.6 0.8 copy-start.5
  101.6 45.0 %copy-start.4 = (s32[16,2]{0,1:T(2,128)S(1)}, s32[16,2]{0,1:T(2,128)}, u32[]{:S(2)}) copy-start(s32[16,2]{0,1:T(2,128)} %param.12) | copy-start | bytes 388
  102.4 52.0 %copy-start.1 = (bf16[16,4096]{1,0:T(8,128)(2,1)S(1)}, bf16[16,4096]{1,0:T(8,128)(2,1)}, u32[]{:S(2)}) copy-start(bf16[16,4096]{1,0:T(8,128)(2,1)} %param.9) | copy-start | bytes 393220
  102.4 52.4 %copy-start.3 = (f32[4096]{0:T(1024)S(1)}, f32[4096]{0:T(1024)}, u32[]{:S(2)}) copy-start(f32[4096]{0:T(1024)} %param.16) | copy-start | bytes 49156
  143.0 10.2 %all-to-all-start.1 = ((bf16[4,12,4096]{2,1,0:T(8,128)(2,1)}), bf16[4,12,4096]{2,1,0:T(8,128)(2,1)S(1)}, u32[]{:S(2)}, u32[]{:S(2)}) async-start(bf16[4,12,4096]{2,1,0:T(8,128)(2,1)} %reshape.89), calls=%async_computation.2 | async-start | bytes 1048576 | tf_op jit(solution)/shard_map/all_to_all | solution.py:61
  146.6 30.6 %all-gather.5.cloned.1.call-start = ((), (), s32[]{:S(2)}) async-start(), calls=%async_computation.5 | async-start | bytes 1179648 | tf_op jit(solution)/shard_map/all_gather | solution.py:72
  154.8 30.0 %copy-start.2 = (bf16[16,4096]{1,0:T(8,128)(2,1)}, bf16[16,4096]{1,0:T(8,128)(2,1)S(1)}, u32[]{:S(2)}) copy-start(bf16[16,4096]{1,0:T(8,128)(2,1)S(1)} %get-tuple-element.10) | copy-start | bytes 393220
  178.9 5.2 %collective-permute-start = (bf16[128,256]{1,0:T(8,128)(2,1)S(1)}, bf16[128,256]{1,0:T(8,128)(2,1)S(1)}, u32[]{:S(2)}, u32[]{:S(2)}) collective-permute-start(bf16[128,256]{1,0:T(8,128)(2,1)S(1)} %convolution_convert_fusion.1), channel_id=1, source_target_pairs={{0,8},{8,16},{16,24},{24,0},{1,9},{9,17},{17,25},{25,1},{2,10},{10... | collective-permute-start | bytes 196616 | tf_op jit(solution)/shard_map/ppermute | solution.py:12
Sparse Core Ops, SparseCore 0:
  25.7 37.9 all-gather.2
  101.8 39.2 reduce-scatter.1
  155.7 21.4 all-gather.4
where the time goes:
time: 192 us; the launch traced here: 191 us
  waiting for transfers between devices  109 us (57%)
  matrix products  40.3 us (21%)
  between operations  13.9 us (7%)
  blocking collectives  13.5 us (7%)
  local copies, waits for them, and re-layouts  6.24 us (3%)
  starting transfers between devices  5.26 us (3%)
  other arithmetic  3.58 us (2%)
    reduce_scatter x1, waiting for transfers between devices, body(): lax.psum_scatter(jnp.dot(block_rows, down_weight, preferred_element_type=...  38.6 us
    all_gather x1, waiting for transfers between devices, body(): block_rows = lax.all_gather(inbound, 'mp', axis=0, tiled=True)  38 us
    dot_general x1, matrix products, body(): jnp.dot(block_rows, down_weight, preferred_element_type=jnp.float32)  25 us
    all_gather x1, waiting for transfers between devices, body(): lax.all_gather(attn_input, 'mp', axis=0, tiled=True)  21.7 us
    all_to_all x1, blocking collectives, body(): lax.all_to_all(buffer, 'section', split_axis=0, concat_axis=0, tiled=True)  13.5 us
    dot_general x1, matrix products, body(): jnp.dot(block_rows, gate_weight, preferred_element_type=jnp.float32)  12.9 us
    all_to_all x1, waiting for transfers between devices, body(): lax.all_to_all(results, 'section', split_axis=0, concat_axis=0, tiled=True)  6.54 us
  transfers between devices with their start and end apart: 5, of which 5 were waited for; matrix products, arithmetic and copies ran while one was open for 0% of the time, Pallas kernels for 0%

commit v1 on v0

--- a/solution.py
+++ b/solution.py
@@ -4,6 +4,18 @@
 from jax.sharding import PartitionSpec as P
 
 epsilon = 1e-05
+
+
+def doubled_up(array, axis, dim):
+    ways, here, step = (lax.axis_size(axis), lax.axis_index(axis), array.shape[dim])
+    line, have = (array, 1)
+    while have < ways:
+        line = jnp.concatenate(
+            [line, lax.ppermute(line, axis, [(d, (d - have) % ways) for d in range(ways)])],
+            axis=dim,
+        )
+        have = 2 * have
+    return jnp.roll(line, here * step, axis=dim)
 
 
 def shifted(value, axis, steps):
@@ -69,9 +81,7 @@
     stream_out = updated.astype(jnp.bfloat16)
     attn_input = normalize(stream_out, attn_gain).astype(jnp.bfloat16)
     kv_local = jnp.dot(
-        lax.all_gather(attn_input, "mp", axis=0, tiled=True),
-        w_kv,
-        preferred_element_type=jnp.float32,
+        doubled_up(attn_input, "mp", 0), w_kv, preferred_element_type=jnp.float32
     ).astype(jnp.bfloat16)
     kv_decode = shifted(kv_local, "section", 1)
     return (stream_out, kv_decode)

time: 192 us -> 212 us (1.10)
  waiting for transfers between devices: 109 us -> 120 us
  local copies, waits for them, and re-layouts: 6.24 us -> 11.3 us
  starting transfers between devices: 5.26 us -> 7.84 us
    ppermute x0 -> x3, waiting for transfers between devices: none -> 33.5 us  [doubled_up(): lax.ppermute(line, axis, [(d, (d - have) % ways) for d in range(ways)])]
    all_gather x1 -> x0, waiting for transfers between devices: 21.7 us -> none  [body(): lax.all_gather(attn_input, 'mp', axis=0, tiled=True)]
    unnamed x14 -> x20, local copies, waits for them, and re-layouts: 2.28 us -> 6.54 us
    ppermute x0 -> x3, starting transfers between devices: none -> 2.64 us  [doubled_up(): lax.ppermute(line, axis, [(d, (d - have) % ways) for d in range(ways)])]
  transfers between devices with their start and end apart: 5 -> 7, of which waited for: 5 -> 7; matrix products, arithmetic and copies ran while one was open for 0% -> 1% of each run, Pallas kernels for 0% -> 0%
where the time goes in v1:
time: 212 us; the launch traced here: 211 us
  waiting for transfers between devices  120 us (57%)
  matrix products  40.3 us (19%)
  between operations  14.2 us (7%)
  blocking collectives  13.5 us (6%)
  local copies, waits for them, and re-layouts  11.3 us (5%)
  starting transfers between devices  7.84 us (4%)
  other arithmetic  3.64 us (2%)
    reduce_scatter x1, waiting for transfers between devices, body(): lax.psum_scatter(jnp.dot(block_rows, down_weight, preferred_element_type=...  38.6 us
    all_gather x1, waiting for transfers between devices, body(): block_rows = lax.all_gather(inbound, 'mp', axis=0, tiled=True)  38 us
    ppermute x3, waiting for transfers between devices, doubled_up(): lax.ppermute(line, axis, [(d, (d - have) % ways) for d in range(ways)])  33.5 us
    dot_general x1, matrix products, body(): jnp.dot(block_rows, down_weight, preferred_element_type=jnp.float32)  25.1 us
    all_to_all x1, blocking collectives, body(): lax.all_to_all(buffer, 'section', split_axis=0, concat_axis=0, tiled=True)  13.5 us
    dot_general x1, matrix products, body(): jnp.dot(block_rows, gate_weight, preferred_element_type=jnp.float32)  12.9 us
    unnamed x20, local copies, waits for them, and re-layouts  6.54 us
    all_to_all x1, waiting for transfers between devices, body(): lax.all_to_all(results, 'section', split_axis=0, concat_axis=0, tiled=True)  6.52 us
  transfers between devices with their start and end apart: 7, of which 7 were waited for; matrix products, arithmetic and copies ran while one was open for 1% of the time, Pallas kernels for 0%

profile of v1, /device:TPU:0, one launch (start us, length us, event | category | flops | bytes accessed | tf_op | source)
XLA Modules:
  0.0 211.2 jit_solution(14694533711070442002)
XLA Ops:
  7.2 0.9 copy.21
  8.3 1.1 fusion.22
  9.6 1.0 fusion.24
  11.2 13.5 %all_to_all.10 = bf16[4,12,4096]{2,1,0:T(8,128)(2,1)S(1)} all-to-all(bf16[4,12,4096]{2,1,0:T(8,128)(2,1)S(1)} %convolution_convert_fusion), channel_id=1, replica_groups=mesh['section'=4,'mp'=8] {'section'}, dimensions={0} | all-to-all | bytes 786432 | tf_op jit(solution)/shard_map/all_to_all | solution.py:56
  24.7 0.8 reshape.88
  25.6 38.0 %all-gather.2.cloned.1.call-done = bf16[384,4096]{1,0:T(8,128)(2,1)} async-done(((bf16[48,4096]{1,0:T(8,128)(2,1)}), bf16[384,4096]{1,0:T(8,128)(2,1)}) %all-gather.2.cloned.1.call-update) | async-done | bytes 3145744 | tf_op jit(solution)/shard_map/all_gather | solution.py:61
  63.7 12.9 %fusion.4 = f32[384,1792]{1,0:T(8,128)} fusion(bf16[384,4096]{1,0:T(8,128)(2,1)} %all-gather.2.cloned.1.call-done, bf16[1,4096,1792]{2,1,0:T(8,128)(2,1)} %param.13), kind=kOutput, calls=%fused_computation.4 | convolution fusion | flops 5637144576 | bytes 20578304 | tf_op jit(solution)/shard_map/dot_general | solution.py:62
  76.6 25.1 %fusion.6 = bf16[384,4096]{1,0:T(8,128)(2,1)} fusion(bf16[1,1792,4096]{2,1,0:T(8,128)(2,1)} %param.15, bf16[384,4096]{1,0:T(8,128)(2,1)} %all-gather.2.cloned.1.call-done, bf16[1,4096,1792]{2,1,0:T(8,128)(2,1)} %param.14, f32[384,1792]{1,0:T(8,128)} %fusion.4), kind=kOutput, calls=%fused_computation.6 | convolution fusion | flops 11279990784 | bytes 38404096 | tf_op jit(solution)/shard_map/dot_general | solution.py:67
  101.7 0.7 copy-done.5
  102.5 38.6 %reduce-scatter.2.cloned.1.call-done = bf16[48,4096]{1,0:T(8,128)(2,1)} async-done(((bf16[384,4096]{1,0:T(8,128)(2,1)}), bf16[48,4096]{1,0:T(8,128)(2,1)}) %reduce-scatter.2.cloned.1.call-update) | async-done | bytes 393232 | tf_op jit(solution)/shard_map/reduce_scatter | solution.py:66
  141.1 1.9 reshape.89
  143.0 3.6 %all-to-all-start.1 = ((bf16[4,12,4096]{2,1,0:T(8,128)(2,1)}), bf16[4,12,4096]{2,1,0:T(8,128)(2,1)S(1)}, u32[]{:S(2)}, u32[]{:S(2)}) async-start(bf16[4,12,4096]{2,1,0:T(8,128)(2,1)} %reshape.89), calls=%async_computation.2 | async-start | bytes 1048576 | tf_op jit(solution)/shard_map/all_to_all | solution.py:73
  146.7 6.5 %all-to-all-done.1 = bf16[4,12,4096]{2,1,0:T(8,128)(2,1)S(1)} async-done(((bf16[4,12,4096]{2,1,0:T(8,128)(2,1)}), bf16[4,12,4096]{2,1,0:T(8,128)(2,1)S(1)}, u32[]{:S(2)}, u32[]{:S(2)}) %all-to-all-start.1) | async-done | bytes 393248 | tf_op jit(solution)/shard_map/all_to_all | solution.py:73
  154.8 0.8 constant_dynamic-update-slice_fusion.7
  155.6 2.5 %collective-permute-start = (bf16[16,4096]{1,0:T(8,128)(2,1)S(1)}, bf16[16,4096]{1,0:T(8,128)(2,1)S(1)}, u32[]{:S(2)}, u32[]{:S(2)}) collective-permute-start(bf16[16,4096]{1,0:T(8,128)(2,1)S(1)} %get-tuple-element.3), channel_id=1, source_target_pairs={{0,7},{1,0},{2,1},{3,2},{4,3},{5,4},{6,5},{7,6},{8,15},{9,8},{10,9... | collective-permute-start | bytes 393224 | tf_op jit(solution)/shard_map/ppermute | solution.py:14
  158.1 2.5 %collective-permute-done = bf16[16,4096]{1,0:T(8,128)(2,1)S(1)} collective-permute-done((bf16[16,4096]{1,0:T(8,128)(2,1)S(1)}, bf16[16,4096]{1,0:T(8,128)(2,1)S(1)}, u32[]{:S(2)}, u32[]{:S(2)}) %collective-permute-start) | collective-permute-done | bytes 131104 | tf_op jit(solution)/shard_map/ppermute | solution.py:14
  160.7 6.4 %collective-permute-done.1 = bf16[32,4096]{1,0:T(8,128)(2,1)S(1)} collective-permute-done((bf16[32,4096]{1,0:T(8,128)(2,1)S(1)}, bf16[32,4096]{1,0:T(8,128)(2,1)S(1)}, u32[]{:S(2)}, u32[]{:S(2)}) %collective-permute-start.1) | collective-permute-done | bytes 262176 | tf_op jit(solution)/shard_map/ppermute | solution.py:14
  168.6 24.5 %collective-permute-done.2 = bf16[64,4096]{1,0:T(8,128)(2,1)S(1)} collective-permute-done((bf16[64,4096]{1,0:T(8,128)(2,1)S(1)}, bf16[64,4096]{1,0:T(8,128)(2,1)S(1)}, u32[]{:S(2)}, u32[]{:S(2)}) %collective-permute-start.2) | collective-permute-done | bytes 524320 | tf_op jit(solution)/shard_map/ppermute | solution.py:14
  193.1 0.8 constant_dynamic-update-slice_fusion.4
  195.3 0.7 constant_dynamic-update-slice_fusion.1
  196.0 0.8 constant_dynamic-update-slice_fusion
  196.9 1.7 convolution_convert_fusion.1
  198.5 1.5 collective-permute-start.3
  200.0 3.7 %collective-permute-done.3 = bf16[128,256]{1,0:T(8,128)(2,1)S(1)} collective-permute-done((bf16[128,256]{1,0:T(8,128)(2,1)S(1)}, bf16[128,256]{1,0:T(8,128)(2,1)S(1)}, u32[]{:S(2)}, u32[]{:S(2)}) %collective-permute-start.3) | collective-permute-done | bytes 65568 | tf_op jit(solution)/shard_map/ppermute | solution.py:24
  (42 shorter events, 6.4 us)
Async XLA Ops:
  7.2 189.7 %copy-start = (bf16[4096,256]{1,0:T(8,128)(2,1)S(1)}, bf16[4096,256]{1,0:T(8,128)(2,1)}, u32[]{:S(2)}) copy-start(bf16[4096,256]{1,0:T(8,128)(2,1)} %param.17) | copy-start | bytes 6291460
  7.2 56.5 %all-gather.2.cloned.1.call-start = ((), (), s32[]{:S(2)}) async-start(), calls=%async_computation.3 | async-start | bytes 3538944 | tf_op jit(solution)/shard_map/all_gather | solution.py:61
  25.6 115.5 %reduce-scatter.2.cloned.1.call-start = ((), (), s32[]{:S(2)}) async-start(), calls=%async_computation.4 | async-start | bytes 3538944 | tf_op jit(solution)/shard_map/reduce_scatter | solution.py:66
  101.6 0.8 copy-start.5
  101.6 45.0 %copy-start.4 = (s32[16,2]{0,1:T(2,128)S(1)}, s32[16,2]{0,1:T(2,128)}, u32[]{:S(2)}) copy-start(s32[16,2]{0,1:T(2,128)} %param.12) | copy-start | bytes 388
  102.4 52.0 %copy-start.1 = (bf16[16,4096]{1,0:T(8,128)(2,1)S(1)}, bf16[16,4096]{1,0:T(8,128)(2,1)}, u32[]{:S(2)}) copy-start(bf16[16,4096]{1,0:T(8,128)(2,1)} %param.9) | copy-start | bytes 393220
  102.5 52.3 %copy-start.3 = (f32[4096]{0:T(1024)S(1)}, f32[4096]{0:T(1024)}, u32[]{:S(2)}) copy-start(f32[4096]{0:T(1024)} %param.16) | copy-start | bytes 49156
  143.0 10.2 %all-to-all-start.1 = ((bf16[4,12,4096]{2,1,0:T(8,128)(2,1)}), bf16[4,12,4096]{2,1,0:T(8,128)(2,1)S(1)}, u32[]{:S(2)}, u32[]{:S(2)}) async-start(bf16[4,12,4096]{2,1,0:T(8,128)(2,1)} %reshape.89), calls=%async_computation.2 | async-start | bytes 1048576 | tf_op jit(solution)/shard_map/all_to_all | solution.py:73
  154.8 42.1 %copy-start.2 = (bf16[16,4096]{1,0:T(8,128)(2,1)}, bf16[16,4096]{1,0:T(8,128)(2,1)S(1)}, u32[]{:S(2)}) copy-start(bf16[16,4096]{1,0:T(8,128)(2,1)S(1)} %get-tuple-element.12) | copy-start | bytes 393220
  155.6 5.0 %collective-permute-start = (bf16[16,4096]{1,0:T(8,128)(2,1)S(1)}, bf16[16,4096]{1,0:T(8,128)(2,1)S(1)}, u32[]{:S(2)}, u32[]{:S(2)}) collective-permute-start(bf16[16,4096]{1,0:T(8,128)(2,1)S(1)} %get-tuple-element.3), channel_id=1, source_target_pairs={{0,7},{1,0},{2,1},{3,2},{4,3},{5,4},{6,5},{7,6},{8,15},{9,8},{10,9... | collective-permute-start | bytes 393224 | tf_op jit(solution)/shard_map/ppermute | solution.py:14
  160.6 6.5 %collective-permute-start.1 = (bf16[32,4096]{1,0:T(8,128)(2,1)S(1)}, bf16[32,4096]{1,0:T(8,128)(2,1)S(1)}, u32[]{:S(2)}, u32[]{:S(2)}) collective-permute-start(bf16[32,4096]{1,0:T(8,128)(2,1)S(1)} %pad_maximum_fusion.1), channel_id=1, source_target_pairs={{0,6},{1,7},{2,0},{3,1},{4,2},{5,3},{6,4},{7,5},{8,14},{9,15},{10,... | collective-permute-start | bytes 786440 | tf_op jit(solution)/shard_map/ppermute | solution.py:14
  167.2 26.0 %collective-permute-start.2 = (bf16[64,4096]{1,0:T(8,128)(2,1)S(1)}, bf16[64,4096]{1,0:T(8,128)(2,1)S(1)}, u32[]{:S(2)}, u32[]{:S(2)}) collective-permute-start(bf16[64,4096]{1,0:T(8,128)(2,1)S(1)} %pad_maximum_fusion), channel_id=1, source_target_pairs={{0,4},{1,5},{2,6},{3,7},{4,0},{5,1},{6,2},{7,3},{8,12},{9,13},{10,... | collective-permute-start | bytes 1572872 | tf_op jit(solution)/shard_map/ppermute | solution.py:14
  198.5 5.2 %collective-permute-start.3 = (bf16[128,256]{1,0:T(8,128)(2,1)S(1)}, bf16[128,256]{1,0:T(8,128)(2,1)S(1)}, u32[]{:S(2)}, u32[]{:S(2)}) collective-permute-start(bf16[128,256]{1,0:T(8,128)(2,1)S(1)} %convolution_convert_fusion.1), channel_id=1, source_target_pairs={{0,8},{8,16},{16,24},{24,0},{1,9},{9,17},{17,25},{25,1},{2,10},{10... | collective-permute-start | bytes 196616 | tf_op jit(solution)/shard_map/ppermute | solution.py:24
Sparse Core Ops, SparseCore 0:
  25.7 37.9 all-gather.1
  101.8 39.2 reduce-scatter.1
